TPU v7x, 256 devices: a whole 4x4x8 slice. The times are simulated.
256 devices in a mesh: gx: 16 (over z, core), gy: 4 (over x), gz: 4 (over y).
Axes of the slice: x: 4, y: 4, z: 8, core: 2. Of those that a mesh axis runs over, the one named last changes fastest.
Arguments:
- velocity: float32 [3, 1024, 128, 512], P(None, 'gx', 'gz', 'gy'), may hold values from -6 to 6
- tile_turbine: int32 [16, 4, 4, 2], P('gx', 'gz', 'gy'), may hold values from 0 to 63
- tile_plane: int32 [16, 4, 4, 2], P('gx', 'gz', 'gy'), may hold values from 0 to 63
- tile_weight: bfloat16 [16, 4, 4, 2, 384, 4096], P('gx', 'gz', 'gy'), may hold values from -0.09375 to 0.09375
- chord: float32 [64, 384], replicated, may hold values from 0.25 to 1
Outputs:
- predicted: float32 [3, 1024, 128, 512], P(None, 'gx', 'gz', 'gy')
- forces: float32 [64, 1152], replicated
All inputs are finite; a program needn't handle non-finite values.
Results may differ from a plain program's by a relative error of at most 0.0032.
Values sent between devices are 32-bit elements; how exact they have to be, the bound alone decides.
No kernel may reach another device: no remote copies, remote signals or barrier semaphores. Data moves between devices by JAX's collectives and lax.ppermute only.
A program may use at most 128 MiB of HBM per device.

v0:
```python
import jax
import jax.numpy as jnp
from jax import lax
from jax.sharding import PartitionSpec as P

DIRS = (-3, -1, -2)


def padded_2(block, sides, width):
    for axis, dim in sides:
        count = lax.axis_size(axis)
        forward = [(i, i + 1) for i in range(count - 1)]
        backward = [(target, source) for source, target in forward]
        low = lax.ppermute(
            lax.slice_in_dim(block, block.shape[dim] - width, None, axis=dim), axis, forward
        )
        high = lax.ppermute(lax.slice_in_dim(block, 0, width, axis=dim), axis, backward)
        block = jnp.concatenate([low, block, high], axis=dim)
    return block


def shifted(p, axis, step):
    idx = [slice(1, -1), slice(1, -1), slice(1, -1)]
    idx[axis + 3] = slice(1 + step, p.shape[axis] - 1 + step)
    lead = [slice(None)] * (p.ndim - 3)
    return p[tuple(lead + idx)]


def strain_viscosity(p):
    grads = [
        [0.5 * (shifted(p[c], DIRS[d], 1) - shifted(p[c], DIRS[d], -1)) for d in range(3)]
        for c in range(3)
    ]
    total = jnp.zeros_like(grads[0][0])
    for c in range(3):
        for d in range(3):
            strain = 0.5 * (grads[c][d] + grads[d][c])
            total = total + strain * strain
    return 0.05 + 1.0 * jnp.sqrt(2.0 * total + 1e-06)


def advance(padded, nu_padded):
    nu_here = shifted(nu_padded, -1, 0)
    result = []
    for c in range(3):
        center = shifted(padded[c], -1, 0)
        advect = jnp.zeros_like(center)
        spread = jnp.zeros_like(center)
        for d in range(3):
            upper = shifted(padded[c], DIRS[d], 1)
            lower = shifted(padded[c], DIRS[d], -1)
            advect = advect + shifted(padded[d], -1, 0) * 0.5 * (upper - lower)
            nu_up = 0.5 * (nu_here + shifted(nu_padded, DIRS[d], 1))
            nu_low = 0.5 * (nu_here + shifted(nu_padded, DIRS[d], -1))
            spread = spread + nu_up * (upper - center) - nu_low * (center - lower)
        result.append(center + 0.25 * (spread - advect))
    return jnp.stack(result)


def actuate(velocity_probe, coef):
    rows = velocity_probe.shape[0]
    parts = velocity_probe.reshape(rows, 3, -1)
    magnitude = jnp.sqrt(jnp.sum(parts * parts, axis=1) + 1e-06)
    return (-2.0 * coef[:, None, :] * magnitude[:, None, :] * parts).reshape(rows, -1)


def body(velocity, tile_turbine, tile_plane, tile_weight, chord):
    cx = velocity.shape[1]
    vertical_coord = velocity.shape[2]
    spanwise_coord = velocity.shape[3]
    tile_count = tile_turbine.shape[3]
    actuator_count = tile_weight.shape[4]
    nturb = chord.shape[0]
    turbine_list = tile_turbine.reshape(tile_count)
    rotor_planes = tile_plane.reshape(tile_count)
    spread_weights = tile_weight.reshape(
        tile_count, actuator_count, vertical_coord * spanwise_coord
    )
    flat = velocity.reshape(3, cx, vertical_coord * spanwise_coord)
    picks = (rotor_planes[:, None] == jnp.arange(cx, dtype=jnp.int32)[None, :]).astype(jnp.float32)
    tiles = jnp.einsum("sx,cxq->scq", picks, flat, precision=lax.Precision.HIGHEST).astype(
        jnp.bfloat16
    )
    block_local = jnp.einsum(
        "spq,scq->scp", spread_weights, tiles, preferred_element_type=jnp.float32
    )
    owning_block = (turbine_list[:, None] == jnp.arange(nturb, dtype=jnp.int32)[None, :]).astype(
        jnp.float32
    )
    partial_sample = jnp.einsum(
        "yr,yw->rw",
        owning_block,
        block_local.reshape(tile_count, -1),
        precision=lax.Precision.HIGHEST,
    )
    sample = lax.psum(partial_sample, ("gx", "gy", "gz"))
    forces = actuate(sample, chord)
    tile_force = jnp.dot(owning_block, forces, precision=lax.Precision.HIGHEST).astype(jnp.bfloat16)
    forces_sent = jnp.einsum(
        "axz,ahx->ahz",
        spread_weights,
        tile_force.reshape(tile_count, 3, actuator_count),
        preferred_element_type=jnp.float32,
    )
    impulse = jnp.einsum(
        "sx,scq->cxq", picks, forces_sent, precision=lax.Precision.HIGHEST
    ).reshape(3, cx, vertical_coord, spanwise_coord)
    padded = padded_2(velocity, (("gx", 1), ("gy", 3), ("gz", 2)), 1)
    viscosity = strain_viscosity(padded)
    nu_padded = padded_2(viscosity, (("gx", 0), ("gy", 2), ("gz", 1)), 1)
    predicted = advance(padded, nu_padded) + impulse
    return (predicted, forces)


def solution(mesh):
    placed = (
        P(None, "gx", "gz", "gy"),
        P("gx", "gz", "gy", None),
        P("gx", "gz", "gy", None),
        P("gx", "gz", "gy", None, None, None),
        P(),
    )
    return jax.shard_map(
        body,
        mesh=mesh,
        in_specs=placed,
        out_specs=(P(None, "gx", "gz", "gy"), P()),
        check_vma=False,
    )
```

profile of v0, /device:TPU:32, one launch (start us, length us, event | category | flops | bytes accessed | tf_op | source)
XLA Modules:
  0.0 375.6 jit_solution(18153228875391277242)
XLA Ops:
  7.2 0.8 fusion.30
  8.0 1.9 collective-permute-start
  10.0 3.6 collective-permute-start.1
  13.6 2.9 reshape.28
  16.5 1.1 convolution_convert_fusion
  17.7 4.7 %fusion.4 = f32[1,2,3,384]{3,2,1,0:T(4,128)S(1)} fusion(bf16[1,1,1,2,384,4096]{5,4,3,2,1,0:T(8,128)(2,1)} %param.8, bf16[2,3,4096]{2,0,1:T(2,128)(2,1)S(1)} %convolution_convert_fusion), kind=kOutput, calls=%fused_computation.11 | convolution fusion | flops 18874368 | bytes 6349824 | tf_op jit(solution)/shard_map/spq,scq->scp/dot_general | solution.py:84
  22.7 3.9 %fusion.29 = (f32[3,66,32,1]{3,2,1,0:T(8,128)}, f32[3,66,32,1]{3,2,1,0:T(8,128)}) fusion(f32[3,66,32,128]{3,2,1,0:T(8,128)S(1)} %constant_dynamic-update-slice_fusion), kind=kLoop, calls=%fused_computation.83 | loop fusion | bytes 101376 | tf_op jit(solution)/shard_map/slice | solution.py:15
  26.6 2.8 copy.27
  29.4 3.4 collective-permute-start.2
  32.8 2.8 copy.28
  35.6 1.3 collective-permute-start.3
  36.9 1.1 fusion.24
  38.1 2.7 copy.29
  40.8 0.8 collective-permute-done.3
  41.6 2.7 copy.30
  44.3 4.0 %pad_maximum_fusion.22 = (f32[3,66,1,130]{3,2,1,0:T(1,128)}, f32[3,66,1,130]{3,2,1,0:T(1,128)}) fusion(f32[3,66,32,1]{3,2,1,0:T(8,128)} %copy.30, f32[3,66,32,128]{3,2,1,0:T(8,128)S(1)} %constant_dynamic-update-slice_fusion, f32[3,66,32,1]{3,2,1,0:T(8,128)} %copy.29), kind=kLoop, calls=%fused_computation.61 | loop fusion | flops 102960 | bytes 3500640 | tf_op jit(solution)/shard_map/slice | solution.py:15
  48.3 4.2 %collective-permute-start.4 = (f32[3,66,1,130]{3,2,1,0:T(1,128)}, f32[3,66,1,130]{3,2,1,0:T(1,128)}, u32[]{:S(2)}, u32[]{:S(2)}) collective-permute-start(f32[3,66,1,130]{3,2,1,0:T(1,128)} %get-tuple-element.6), channel_id=1, source_target_pairs={{0,1},{1,2},{2,3},{4,5},{5,6},{6,7},{8,9},{9,10},{10,11},{12,13},{... | collective-permute-start | bytes 308888 | tf_op jit(solution)/shard_map/ppermute | solution.py:14
  52.4 1.5 collective-permute-start.5
  53.9 235.0 %all-reduce.2.cloned.1.call-done = f32[64,1152]{1,0:T(8,128)} async-done(((f32[64,1152]{1,0:T(8,128)}), f32[64,1152]{1,0:T(8,128)}) %all-reduce.2.cloned.1.call-update) | async-done | bytes 294928 | tf_op jit(solution)/shard_map/psum | solution.py:96
  288.9 1.9 mul.296
  290.8 1.8 mul.297
  292.6 1.9 reduce_sum.9
  294.5 1.0 sqrt_multiply_fusion
  295.7 6.0 %pad_maximum_fusion = f32[3,66,34,130]{3,2,1,0:T(8,128)S(1)} fusion(f32[3,66,1,130]{3,2,1,0:T(1,128)} %collective-permute-done.5, f32[3,66,32,1]{3,2,1,0:T(8,128)} %copy.30, f32[3,66,32,128]{3,2,1,0:T(8,128)S(1)} %constant_dynamic-update-slice_fusion, f32[3,66,32,1]{3,2,1,0:T(8,128)} %copy.29, f32[3,66,1,130]{3,2,1,0:T(1,128)} %collective-permute-done.4), kind=kLoop, calls=%fused_computation | loop fusion | flops 3500640 | bytes 7001280 | tf_op jit(solution)/shard_map/concatenate | solution.py:18
  302.2 4.8 %sqrt_add_fusion = f32[64,32,128]{2,1,0:T(8,128)S(1)} fusion(f32[66,34,130]{2,1,0:T(8,128)S(1)} %get-tuple-element.10, f32[66,34,130]{2,1,0:T(8,128)S(1)} %get-tuple-element.8, f32[66,34,130]{2,1,0:T(8,128)S(1)} %get-tuple-element.9), kind=kLoop, calls=%fused_computation.46 | loop fusion | flops 9961472 | bytes 19922944 | tf_op jit(solution)/shard_map/add | solution.py:39
  307.1 1.0 copy-done.4
  308.1 3.5 collective-permute-start.6
  311.6 1.9 collective-permute-start.7
  313.8 2.8 collective-permute-done.7
  316.7 1.3 pad_maximum_fusion.1
  318.0 1.7 fusion.31
  319.7 1.9 copy.31
  321.6 1.3 collective-permute-start.8
  322.9 1.9 copy.33
  324.7 4.5 %collective-permute-start.9 = (f32[66,32,1]{0,1,2:T(8,128)S(1)}, f32[66,32,1]{0,1,2:T(8,128)S(1)}, u32[]{:S(2)}, u32[]{:S(2)}) collective-permute-start(f32[66,32,1]{0,1,2:T(8,128)S(1)} %copy.33), channel_id=1, source_target_pairs={{0,4},{4,8},{8,12},{1,5},{5,9},{9,13},{2,6},{6,10},{10,14},{3,7},{... | collective-permute-start | bytes 25352 | tf_op jit(solution)/shard_map/ppermute | solution.py:14
  329.3 3.7 fusion
  333.0 1.9 copy.32
  334.9 1.9 copy.34
  336.8 1.9 pad_maximum_fusion.23
  338.6 1.3 collective-permute-start.10
  339.9 4.8 %collective-permute-start.11 = (f32[66,1,130]{2,1,0:T(1,128)S(1)}, f32[66,1,130]{2,1,0:T(1,128)S(1)}, u32[]{:S(2)}, u32[]{:S(2)}) collective-permute-start(f32[66,1,130]{2,1,0:T(1,128)S(1)} %get-tuple-element.11), channel_id=1, source_target_pairs={{0,1},{1,2},{2,3},{4,5},{5,6},{6,7},{8,9},{9,10},{10,11},{12,13},{... | collective-permute-start | bytes 102968 | tf_op jit(solution)/shard_map/ppermute | solution.py:14
  344.7 1.5 fusion.19
  346.9 1.2 copy-done.1
  348.1 0.8 copy-done.3
  348.9 5.8 %add_bitcast_fusion.2 = f32[1,64,32,128]{3,2,1,0:T(8,128)S(1)} fusion(f32[66,34,130]{2,1,0:T(8,128)S(1)} %copy-done.3, f32[66,34,130]{2,1,0:T(8,128)S(1)} %get-tuple-element.8, f32[66,34,130]{2,1,0:T(8,128)S(1)} %copy-done.1, f32[64,32,128]{2,1,0:T(8,128)S(1)} %copy-done.5, f32[1,32,128]{2,1,0:T(8,128)S(1)} %collective-permute-done.6, ...), kind=kLoop, calls=%fused_computation.45 | loop fusion | flops 15990784 | bytes 11652640 | tf_op jit(solution)/shard_map/stack | solution.py:57
  354.7 5.8 %add_bitcast_fusion.1 = f32[1,64,32,128]{3,2,1,0:T(8,128)S(1)} fusion(f32[66,34,130]{2,1,0:T(8,128)S(1)} %get-tuple-element.8, f32[66,34,130]{2,1,0:T(8,128)S(1)} %copy-done.3, f32[66,34,130]{2,1,0:T(8,128)S(1)} %copy-done.1, f32[64,32,128]{2,1,0:T(8,128)S(1)} %copy-done.5, f32[1,32,128]{2,1,0:T(8,128)S(1)} %collective-permute-done.6, ...), kind=kLoop, calls=%fused_computation.44 | loop fusion | flops 15990784 | bytes 11652640 | tf_op jit(solution)/shard_map/stack | solution.py:57
  360.5 5.8 %add_bitcast_fusion = f32[1,64,32,128]{3,2,1,0:T(8,128)S(1)} fusion(f32[66,34,130]{2,1,0:T(8,128)S(1)} %copy-done.1, f32[66,34,130]{2,1,0:T(8,128)S(1)} %copy-done.3, f32[66,34,130]{2,1,0:T(8,128)S(1)} %get-tuple-element.8, f32[64,32,128]{2,1,0:T(8,128)S(1)} %copy-done.5, f32[1,32,128]{2,1,0:T(8,128)S(1)} %collective-permute-done.6, ...), kind=kLoop, calls=%fused_computation.43 | loop fusion | flops 15990784 | bytes 11652640 | tf_op jit(solution)/shard_map/stack | solution.py:57
  366.4 2.4 bitcast_add_fusion
  (47 shorter events, 1.9 us)
Async XLA Ops:
  7.2 281.8 %all-reduce.2.cloned.1.call-start = ((), (), s32[]{:S(2)}) async-start(), calls=%async_computation | async-start | bytes 589824 | tf_op jit(solution)/shard_map/psum | solution.py:96
  8.0 14.3 %collective-permute-start = (f32[3,1,32,128]{3,2,1,0:T(8,128)S(1)}, f32[3,1,32,128]{3,2,1,0:T(8,128)S(1)}, u32[]{:S(2)}, u32[]{:S(2)}) collective-permute-start(f32[3,1,32,128]{3,2,1,0:T(8,128)S(1)} %get-tuple-element.16), channel_id=1, source_target_pairs={{0,16},{16,32},{32,48},{48,64},{64,80},{80,96},{96,112},{112,128},... | collective-permute-start | bytes 147464 | tf_op jit(solution)/shard_map/ppermute | solution.py:14
  10.0 6.6 %copy-start.12 = (s32[1,1,1,2]{3,2,1,0:T(1,128)S(1)}, s32[1,1,1,2]{3,2,1,0:T(1,128)}, u32[]{:S(2)}) copy-start(s32[1,1,1,2]{3,2,1,0:T(1,128)} %param.7) | copy-start | bytes 28
  10.0 12.7 %collective-permute-start.1 = (f32[3,1,32,128]{3,2,1,0:T(8,128)S(1)}, f32[3,1,32,128]{3,2,1,0:T(8,128)S(1)}, u32[]{:S(2)}, u32[]{:S(2)}) collective-permute-start(f32[3,1,32,128]{3,2,1,0:T(8,128)S(1)} %get-tuple-element.15), channel_id=1, source_target_pairs={{16,0},{32,16},{48,32},{64,48},{80,64},{96,80},{112,96},{128,112},... | collective-permute-start | bytes 147464 | tf_op jit(solution)/shard_map/ppermute | solution.py:17
  17.6 4.7 %copy-start.8 = (f32[3,64,32,128]{3,2,1,0:T(8,128)S(1)}, f32[3,64,32,128]{3,2,1,0:T(8,128)}, u32[]{:S(2)}) copy-start(f32[3,64,32,128]{3,2,1,0:T(8,128)} %param.5) | copy-start | bytes 9437188
  26.6 10.3 %copy-start.11 = (s32[1,1,1,2]{3,2,1,0:T(1,128)S(1)}, s32[1,1,1,2]{3,2,1,0:T(1,128)}, u32[]{:S(2)}) copy-start(s32[1,1,1,2]{3,2,1,0:T(1,128)} %param.6) | copy-start | bytes 28
  29.4 8.7 %collective-permute-start.2 = (f32[3,66,32,1]{1,2,3,0:T(8,128)S(1)}, f32[3,66,32,1]{1,2,3,0:T(8,128)S(1)}, u32[]{:S(2)}, u32[]{:S(2)}) collective-permute-start(f32[3,66,32,1]{1,2,3,0:T(8,128)S(1)} %copy.27), channel_id=1, source_target_pairs={{0,4},{4,8},{8,12},{1,5},{5,9},{9,13},{2,6},{6,10},{10,14},{3,7},{... | collective-permute-start | bytes 76040 | tf_op jit(solution)/shard_map/ppermute | solution.py:14
  35.6 6.0 %collective-permute-start.3 = (f32[3,66,32,1]{1,2,3,0:T(8,128)S(1)}, f32[3,66,32,1]{1,2,3,0:T(8,128)S(1)}, u32[]{:S(2)}, u32[]{:S(2)}) collective-permute-start(f32[3,66,32,1]{1,2,3,0:T(8,128)S(1)} %copy.28), channel_id=1, source_target_pairs={{4,0},{8,4},{12,8},{5,1},{9,5},{13,9},{6,2},{10,6},{14,10},{7,3},{... | collective-permute-start | bytes 76040 | tf_op jit(solution)/shard_map/ppermute | solution.py:17
  48.3 247.4 %collective-permute-start.4 = (f32[3,66,1,130]{3,2,1,0:T(1,128)}, f32[3,66,1,130]{3,2,1,0:T(1,128)}, u32[]{:S(2)}, u32[]{:S(2)}) collective-permute-start(f32[3,66,1,130]{3,2,1,0:T(1,128)} %get-tuple-element.6), channel_id=1, source_target_pairs={{0,1},{1,2},{2,3},{4,5},{5,6},{6,7},{8,9},{9,10},{10,11},{12,13},{... | collective-permute-start | bytes 308888 | tf_op jit(solution)/shard_map/ppermute | solution.py:14
  52.4 243.2 %collective-permute-start.5 = (f32[3,66,1,130]{3,2,1,0:T(1,128)}, f32[3,66,1,130]{3,2,1,0:T(1,128)}, u32[]{:S(2)}, u32[]{:S(2)}) collective-permute-start(f32[3,66,1,130]{3,2,1,0:T(1,128)} %get-tuple-element.7), channel_id=1, source_target_pairs={{1,0},{2,1},{3,2},{5,4},{6,5},{7,6},{9,8},{10,9},{11,10},{13,12},{... | collective-permute-start | bytes 308888 | tf_op jit(solution)/shard_map/ppermute | solution.py:17
  288.9 6.6 %copy-start.9 = (f32[64,1152]{1,0:T(8,128)S(1)}, f32[64,1152]{1,0:T(8,128)}, u32[]{:S(2)}) copy-start(f32[64,1152]{1,0:T(8,128)} %all-reduce.2.cloned.1.call-done) | copy-start | bytes 884740
  295.6 17.9 %copy-start.10 = (f32[64,1152]{1,0:T(8,128)}, f32[64,1152]{1,0:T(8,128)S(1)}, u32[]{:S(2)}) copy-start(f32[64,1152]{1,0:T(8,128)S(1)} %mul.301) | copy-start | bytes 884740
  302.2 4.8 %copy-start = (f32[66,34,130]{2,1,0:T(8,128)}, f32[66,34,130]{2,1,0:T(8,128)S(1)}, u32[]{:S(2)}) copy-start(f32[66,34,130]{2,1,0:T(8,128)S(1)} %get-tuple-element.9) | copy-start | bytes 3500644
  302.2 4.8 %copy-start.2 = (f32[66,34,130]{2,1,0:T(8,128)}, f32[66,34,130]{2,1,0:T(8,128)S(1)}, u32[]{:S(2)}) copy-start(f32[66,34,130]{2,1,0:T(8,128)S(1)} %get-tuple-element.10) | copy-start | bytes 3500644
  307.1 1.0 copy-start.4
  308.1 5.8 %collective-permute-start.6 = (f32[1,32,128]{2,1,0:T(8,128)S(1)}, f32[1,32,128]{2,1,0:T(8,128)S(1)}, u32[]{:S(2)}, u32[]{:S(2)}) collective-permute-start(f32[1,32,128]{2,1,0:T(8,128)S(1)} %get-tuple-element.20), channel_id=1, source_target_pairs={{16,0},{32,16},{48,32},{64,48},{80,64},{96,80},{112,96},{128,112},... | collective-permute-start | bytes 49160 | tf_op jit(solution)/shard_map/ppermute | solution.py:17
  311.6 5.1 %collective-permute-start.7 = (f32[1,32,128]{2,1,0:T(8,128)S(1)}, f32[1,32,128]{2,1,0:T(8,128)S(1)}, u32[]{:S(2)}, u32[]{:S(2)}) collective-permute-start(f32[1,32,128]{2,1,0:T(8,128)S(1)} %get-tuple-element.19), channel_id=1, source_target_pairs={{0,16},{16,32},{32,48},{48,64},{64,80},{80,96},{96,112},{112,128},... | collective-permute-start | bytes 49160 | tf_op jit(solution)/shard_map/ppermute | solution.py:14
  321.6 11.4 %collective-permute-start.8 = (f32[66,32,1]{0,1,2:T(8,128)S(1)}, f32[66,32,1]{0,1,2:T(8,128)S(1)}, u32[]{:S(2)}, u32[]{:S(2)}) collective-permute-start(f32[66,32,1]{0,1,2:T(8,128)S(1)} %copy.31), channel_id=1, source_target_pairs={{4,0},{8,4},{12,8},{5,1},{9,5},{13,9},{6,2},{10,6},{14,10},{7,3},{... | collective-permute-start | bytes 25352 | tf_op jit(solution)/shard_map/ppermute | solution.py:17
  324.7 10.2 %collective-permute-start.9 = (f32[66,32,1]{0,1,2:T(8,128)S(1)}, f32[66,32,1]{0,1,2:T(8,128)S(1)}, u32[]{:S(2)}, u32[]{:S(2)}) collective-permute-start(f32[66,32,1]{0,1,2:T(8,128)S(1)} %copy.33), channel_id=1, source_target_pairs={{0,4},{4,8},{8,12},{1,5},{5,9},{9,13},{2,6},{6,10},{10,14},{3,7},{... | collective-permute-start | bytes 25352 | tf_op jit(solution)/shard_map/ppermute | solution.py:14
  338.6 8.2 %collective-permute-start.10 = (f32[66,1,130]{2,1,0:T(1,128)S(1)}, f32[66,1,130]{2,1,0:T(1,128)S(1)}, u32[]{:S(2)}, u32[]{:S(2)}) collective-permute-start(f32[66,1,130]{2,1,0:T(1,128)S(1)} %get-tuple-element.12), channel_id=1, source_target_pairs={{1,0},{2,1},{3,2},{5,4},{6,5},{7,6},{9,8},{10,9},{11,10},{13,12},{... | collective-permute-start | bytes 102968 | tf_op jit(solution)/shard_map/ppermute | solution.py:17
  339.9 6.9 %collective-permute-start.11 = (f32[66,1,130]{2,1,0:T(1,128)S(1)}, f32[66,1,130]{2,1,0:T(1,128)S(1)}, u32[]{:S(2)}, u32[]{:S(2)}) collective-permute-start(f32[66,1,130]{2,1,0:T(1,128)S(1)} %get-tuple-element.11), channel_id=1, source_target_pairs={{0,1},{1,2},{2,3},{4,5},{5,6},{6,7},{8,9},{9,10},{10,11},{12,13},{... | collective-permute-start | bytes 102968 | tf_op jit(solution)/shard_map/ppermute | solution.py:14
  344.7 2.2 copy-start.5
  344.7 2.2 copy-start.6
  344.7 2.2 copy-start.7
  346.3 1.8 copy-start.1
  346.3 2.6 copy-start.3
Sparse Core Ops, SparseCore 0:
  38.2 250.7 all-reduce.1
where the time goes:
time: 376 us
  waiting for transfers between devices  239 us (64%)
  other arithmetic  42.5 us (11%)
  local copies, waits for them, and re-layouts  34.3 us (9%)
  starting transfers between devices  33.2 us (9%)
  between operations  14.5 us (4%)
  matrix products  12.4 us (3%)
    psum x1, waiting for transfers between devices, body(): sample = lax.psum(partial_sample, ('gx', 'gy', 'gz'))  235 us
    ppermute x6, starting transfers between devices, padded_2(): lax.ppermute(lax.slice_in_dim(block, block.shape[dim] - width, None, axis...  20.7 us
    another operation x3, other arithmetic, advance(): return jnp.stack(result)  17.4 us
    ppermute x6, starting transfers between devices, padded_2(): lax.ppermute(lax.slice_in_dim(block, 0, width, axis=dim), axis, backward)  12.5 us
    slice x5, local copies, waits for them, and re-layouts, padded_2(): lax.slice_in_dim(block, block.shape[dim] - width, None, axis=dim)  10.3 us
    concatenate x3, other arithmetic, padded_2(): block = jnp.concatenate([low, block, high], axis=dim)  9.16 us
  transfers between devices with their start and end apart: 13, of which 3 were waited for; matrix products, arithmetic and copies ran while one was open for 10% of the time, Pallas kernels for 0%

commit v1 on v0

--- a/solution.py
+++ b/solution.py
@@ -2,6 +2,7 @@
 import jax.numpy as jnp
 from jax import lax
 from jax.sharding import PartitionSpec as P
+from jax.lax import all_gather
 
 DIRS = (-3, -1, -2)
 
@@ -93,7 +94,12 @@
         block_local.reshape(tile_count, -1),
         precision=lax.Precision.HIGHEST,
     )
-    sample = lax.psum(partial_sample, ("gx", "gy", "gz"))
+
+    def rest_the_terms(xx):
+        passed = all_gather(xx, ("gx", "gy", "gz"))
+        return jnp.sum(passed, axis=0)
+
+    sample = rest_the_terms(partial_sample)
     forces = actuate(sample, chord)
     tile_force = jnp.dot(owning_block, forces, precision=lax.Precision.HIGHEST).astype(jnp.bfloat16)
     forces_sent = jnp.einsum(

time: 376 us -> 294 us (0.78); the launches traced: 376 us -> 290 us
  waiting for transfers between devices: 239 us -> 128 us
  other arithmetic: 42.5 us -> 67.9 us
    psum x1 -> x0, waiting for transfers between devices: 235 us -> none  [body(): sample = lax.psum(partial_sample, ('gx', 'gy', 'gz'))]
    all_gather x0 -> x1, waiting for transfers between devices: none -> 108 us  [rest_the_terms(): passed = all_gather(xx, ('gx', 'gy', 'gz'))]
    reduce_sum x0 -> x1, other arithmetic: none -> 23.7 us  [rest_the_terms(): return jnp.sum(passed, axis=0)]
    ppermute x6, waiting for transfers between devices: 0.81 us -> 15.5 us  [padded_2(): lax.ppermute(lax.slice_in_dim(block, 0, width, axis=dim), axis, backward)]
    another operation x3, other arithmetic: 17.4 us -> 26.6 us  [advance(): return jnp.stack(result)]
  transfers between devices with their start and end apart: 13 -> 13, of which waited for: 3 -> 8; matrix products, arithmetic and copies ran while one was open for 10% -> 24% of each run, Pallas kernels for 0% -> 0%
where the time goes in v1:
time: 294 us; the launch traced here: 290 us
  waiting for transfers between devices  128 us (44%)
  other arithmetic  67.9 us (23%)
  local copies, waits for them, and re-layouts  34.8 us (12%)
  starting transfers between devices  30.9 us (11%)
  between operations  14.5 us (5%)
  matrix products  14.1 us (5%)
    all_gather x1, waiting for transfers between devices, rest_the_terms(): passed = all_gather(xx, ('gx', 'gy', 'gz'))  108 us
    another operation x3, other arithmetic, advance(): return jnp.stack(result)  26.6 us
    reduce_sum x1, other arithmetic, rest_the_terms(): return jnp.sum(passed, axis=0)  23.7 us
    ppermute x6, starting transfers between devices, padded_2(): lax.ppermute(lax.slice_in_dim(block, block.shape[dim] - width, None, axis...  17.8 us
    ppermute x6, waiting for transfers between devices, padded_2(): lax.ppermute(lax.slice_in_dim(block, 0, width, axis=dim), axis, backward)  15.5 us
    ppermute x6, starting transfers between devices, padded_2(): lax.ppermute(lax.slice_in_dim(block, 0, width, axis=dim), axis, backward)  13.1 us
    slice x5, local copies, waits for them, and re-layouts, padded_2(): lax.slice_in_dim(block, block.shape[dim] - width, None, axis=dim)  10.5 us
    concatenate x3, other arithmetic, padded_2(): block = jnp.concatenate([low, block, high], axis=dim)  6.08 us
  transfers between devices with their start and end apart: 13, of which 8 were waited for; matrix products, arithmetic and copies ran while one was open for 24% of the time, Pallas kernels for 0%

profile of v1, /device:TPU:32, one launch (start us, length us, event | category | flops | bytes accessed | tf_op | source)
XLA Modules:
  0.0 289.8 jit_solution(5761058461444359643)
XLA Ops:
  7.2 4.6 %reshape.28 = f32[3,64,4096]{2,1,0:T(8,128)} reshape(f32[3,64,32,128]{3,2,1,0:T(8,128)} %param.5) | data formatting | bytes 6291456 | tf_op jit(solution)/shard_map/reshape | solution.py:80
  11.8 3.0 %convolution_convert_fusion = bf16[2,3,4096]{2,0,1:T(2,128)(2,1)S(1)} fusion(f32[3,64,4096]{2,1,0:T(8,128)} %reshape.28, s32[2]{0:T(128)S(1)} %bitcast.52), kind=kOutput, calls=%fused_computation.5 | convolution fusion | flops 18899072 | bytes 3194888 | tf_op jit(solution)/shard_map/sx,cxq->scq/dot_general | solution.py:82
  14.8 4.5 %fusion.4 = f32[1,2,3,384]{3,2,1,0:T(4,128)S(1)} fusion(bf16[1,1,1,2,384,4096]{5,4,3,2,1,0:T(8,128)(2,1)} %param.8, bf16[2,3,4096]{2,0,1:T(2,128)(2,1)S(1)} %convolution_convert_fusion), kind=kOutput, calls=%fused_computation.11 | convolution fusion | flops 18874368 | bytes 6349824 | tf_op jit(solution)/shard_map/spq,scq->scp/dot_general | solution.py:85
  19.4 1.1 fusion.24
  20.5 0.8 fusion.30
  21.4 1.9 collective-permute-start
  23.3 3.6 %collective-permute-start.1 = (f32[3,1,32,128]{3,2,1,0:T(8,128)S(1)}, f32[3,1,32,128]{3,2,1,0:T(8,128)S(1)}, u32[]{:S(2)}, u32[]{:S(2)}) collective-permute-start(f32[3,1,32,128]{3,2,1,0:T(8,128)S(1)} %get-tuple-element.15), channel_id=1, source_target_pairs={{16,0},{32,16},{48,32},{64,48},{80,64},{96,80},{112,96},{128,112},... | collective-permute-start | bytes 147464 | tf_op jit(solution)/shard_map/ppermute | solution.py:18
  26.9 2.2 constant_dynamic-update-slice_fusion.1
  29.2 3.9 %fusion.29 = (f32[3,66,32,1]{3,2,1,0:T(8,128)}, f32[3,66,32,1]{3,2,1,0:T(8,128)}) fusion(f32[3,66,32,128]{3,2,1,0:T(8,128)S(1)} %constant_dynamic-update-slice_fusion), kind=kLoop, calls=%fused_computation.83 | loop fusion | bytes 101376 | tf_op jit(solution)/shard_map/slice | solution.py:16
  33.1 2.8 copy.27
  35.9 3.4 %collective-permute-start.2 = (f32[3,66,32,1]{1,2,3,0:T(8,128)S(1)}, f32[3,66,32,1]{1,2,3,0:T(8,128)S(1)}, u32[]{:S(2)}, u32[]{:S(2)}) collective-permute-start(f32[3,66,32,1]{1,2,3,0:T(8,128)S(1)} %copy.27), channel_id=1, source_target_pairs={{0,4},{4,8},{8,12},{1,5},{5,9},{9,13},{2,6},{6,10},{10,14},{3,7},{... | collective-permute-start | bytes 76040 | tf_op jit(solution)/shard_map/ppermute | solution.py:15
  39.3 2.8 copy.28
  42.1 1.3 collective-permute-start.3
  43.4 2.7 copy.29
  46.1 2.2 collective-permute-done.3
  48.3 2.7 copy.30
  50.9 3.9 %pad_maximum_fusion.22 = (f32[3,66,1,130]{3,2,1,0:T(1,128)S(1)}, f32[3,66,1,130]{3,2,1,0:T(1,128)S(1)}) fusion(f32[3,66,32,1]{3,2,1,0:T(8,128)} %copy.30, f32[3,66,32,128]{3,2,1,0:T(8,128)} %copy-done.4, f32[3,66,32,1]{3,2,1,0:T(8,128)} %copy.29), kind=kLoop, calls=%fused_computation.61 | loop fusion | flops 102960 | bytes 3500640 | tf_op jit(solution)/shard_map/slice | solution.py:16
  54.8 3.8 %collective-permute-start.4 = (f32[3,66,1,130]{3,2,1,0:T(1,128)S(1)}, f32[3,66,1,130]{3,2,1,0:T(1,128)S(1)}, u32[]{:S(2)}, u32[]{:S(2)}) collective-permute-start(f32[3,66,1,130]{3,2,1,0:T(1,128)S(1)} %get-tuple-element.6), channel_id=1, source_target_pairs={{0,1},{1,2},{2,3},{4,5},{5,6},{6,7},{8,9},{9,10},{10,11},{12,13},{... | collective-permute-start | bytes 308888 | tf_op jit(solution)/shard_map/ppermute | solution.py:15
  58.6 1.5 collective-permute-start.5
  60.1 3.6 %collective-permute-done.4 = f32[3,66,1,130]{3,2,1,0:T(1,128)S(1)} collective-permute-done((f32[3,66,1,130]{3,2,1,0:T(1,128)S(1)}, f32[3,66,1,130]{3,2,1,0:T(1,128)S(1)}, u32[]{:S(2)}, u32[]{:S(2)}) %collective-permute-start.4) | collective-permute-done | bytes 102992 | tf_op jit(solution)/shard_map/ppermute | solution.py:15
  63.7 4.1 %collective-permute-done.5 = f32[3,66,1,130]{3,2,1,0:T(1,128)S(1)} collective-permute-done((f32[3,66,1,130]{3,2,1,0:T(1,128)S(1)}, f32[3,66,1,130]{3,2,1,0:T(1,128)S(1)}, u32[]{:S(2)}, u32[]{:S(2)}) %collective-permute-start.5) | collective-permute-done | bytes 102992 | tf_op jit(solution)/shard_map/ppermute | solution.py:18
  67.9 4.0 %pad_maximum_fusion = f32[3,66,34,130]{3,2,1,0:T(8,128)S(1)} fusion(f32[3,66,1,130]{3,2,1,0:T(1,128)S(1)} %collective-permute-done.5, f32[3,66,32,1]{3,2,1,0:T(8,128)S(1)} %copy-done.9, f32[3,66,32,128]{3,2,1,0:T(8,128)S(1)} %copy-done.5, f32[3,66,32,1]{3,2,1,0:T(8,128)S(1)} %copy-done.8, f32[3,66,1,130]{3,2,1,0:T(1,128)S(1)} %collective-permute-done.4), kind=kLoop, calls=%fused_computation | loop fusion | flops 3500640 | bytes 7001280 | tf_op jit(solution)/shard_map/concatenate | solution.py:19
  72.4 4.8 %sqrt_add_fusion = f32[64,32,128]{2,1,0:T(8,128)S(1)} fusion(f32[66,34,130]{2,1,0:T(8,128)S(1)} %get-tuple-element.10, f32[66,34,130]{2,1,0:T(8,128)S(1)} %get-tuple-element.8, f32[66,34,130]{2,1,0:T(8,128)S(1)} %get-tuple-element.9), kind=kLoop, calls=%fused_computation.46 | loop fusion | flops 9961472 | bytes 19922944 | tf_op jit(solution)/shard_map/add | solution.py:40
  77.3 1.9 collective-permute-start.7
  79.2 3.6 %collective-permute-start.6 = (f32[1,32,128]{2,1,0:T(8,128)S(1)}, f32[1,32,128]{2,1,0:T(8,128)S(1)}, u32[]{:S(2)}, u32[]{:S(2)}) collective-permute-start(f32[1,32,128]{2,1,0:T(8,128)S(1)} %get-tuple-element.20), channel_id=1, source_target_pairs={{16,0},{32,16},{48,32},{64,48},{80,64},{96,80},{112,96},{128,112},... | collective-permute-start | bytes 49160 | tf_op jit(solution)/shard_map/ppermute | solution.py:18
  82.9 1.4 collective-permute-done.6
  84.3 1.9 fusion.31
  86.3 1.9 copy.33
  88.1 3.4 %collective-permute-start.9 = (f32[66,32,1]{0,1,2:T(8,128)S(1)}, f32[66,32,1]{0,1,2:T(8,128)S(1)}, u32[]{:S(2)}, u32[]{:S(2)}) collective-permute-start(f32[66,32,1]{0,1,2:T(8,128)S(1)} %copy.33), channel_id=1, source_target_pairs={{0,4},{4,8},{8,12},{1,5},{5,9},{9,13},{2,6},{6,10},{10,14},{3,7},{... | collective-permute-start | bytes 25352 | tf_op jit(solution)/shard_map/ppermute | solution.py:15
  91.5 1.9 copy.31
  93.4 1.3 collective-permute-start.8
  94.7 2.0 copy.34
  96.7 2.8 collective-permute-done.8
  99.5 2.0 copy.32
  101.5 2.0 pad_maximum_fusion.23
  103.5 3.4 %collective-permute-start.11 = (f32[66,1,130]{2,1,0:T(1,128)S(1)}, f32[66,1,130]{2,1,0:T(1,128)S(1)}, u32[]{:S(2)}, u32[]{:S(2)}) collective-permute-start(f32[66,1,130]{2,1,0:T(1,128)S(1)} %get-tuple-element.11), channel_id=1, source_target_pairs={{0,1},{1,2},{2,3},{4,5},{5,6},{6,7},{8,9},{9,10},{10,11},{12,13},{... | collective-permute-start | bytes 102968 | tf_op jit(solution)/shard_map/ppermute | solution.py:15
  107.0 1.8 collective-permute-start.10
  108.9 5.0 %collective-permute-done.10 = f32[66,1,130]{2,1,0:T(1,128)S(1)} collective-permute-done((f32[66,1,130]{2,1,0:T(1,128)S(1)}, f32[66,1,130]{2,1,0:T(1,128)S(1)}, u32[]{:S(2)}, u32[]{:S(2)}) %collective-permute-start.10) | collective-permute-done | bytes 34352 | tf_op jit(solution)/shard_map/ppermute | solution.py:18
  113.9 12.4 %add_bitcast_fusion.1 = f32[1,64,32,128]{3,2,1,0:T(8,128)} fusion(f32[66,34,130]{2,1,0:T(8,128)S(1)} %get-tuple-element.8, f32[66,34,130]{2,1,0:T(8,128)} %copy-done.2, f32[66,34,130]{2,1,0:T(8,128)S(1)} %copy-done.1, f32[64,32,128]{2,1,0:T(8,128)} %copy-done.6, f32[1,32,128]{2,1,0:T(8,128)S(1)} %collective-permute-done.6, ...), kind=kLoop, calls=%fused_computation.44 | loop fusion | flops 15990784 | bytes 11652640 | tf_op jit(solution)/shard_map/stack | solution.py:58
  126.4 7.1 %add_bitcast_fusion = f32[1,64,32,128]{3,2,1,0:T(8,128)} fusion(f32[66,34,130]{2,1,0:T(8,128)S(1)} %copy-done.1, f32[66,34,130]{2,1,0:T(8,128)S(1)} %copy-done.3, f32[66,34,130]{2,1,0:T(8,128)S(1)} %get-tuple-element.8, f32[64,32,128]{2,1,0:T(8,128)S(1)} %copy-done.7, f32[1,32,128]{2,1,0:T(8,128)S(1)} %collective-permute-done.6, ...), kind=kLoop, calls=%fused_computation.43 | loop fusion | flops 15990784 | bytes 11652640 | tf_op jit(solution)/shard_map/stack | solution.py:58
  133.5 7.0 %add_bitcast_fusion.2 = f32[1,64,32,128]{3,2,1,0:T(8,128)} fusion(f32[66,34,130]{2,1,0:T(8,128)S(1)} %copy-done.3, f32[66,34,130]{2,1,0:T(8,128)S(1)} %get-tuple-element.8, f32[66,34,130]{2,1,0:T(8,128)S(1)} %copy-done.1, f32[64,32,128]{2,1,0:T(8,128)S(1)} %copy-done.7, f32[1,32,128]{2,1,0:T(8,128)S(1)} %collective-permute-done.6, ...), kind=kLoop, calls=%fused_computation.45 | loop fusion | flops 15990784 | bytes 11652640 | tf_op jit(solution)/shard_map/stack | solution.py:58
  140.5 108.2 %all-gather.3.cloned.1.call-done = f32[16384,1152]{1,0:T(8,128)} async-done(((f32[64,1152]{1,0:T(8,128)}), f32[16384,1152]{1,0:T(8,128)}) %all-gather.3.cloned.1.call-update) | async-done | bytes 75497488 | tf_op jit(solution)/shard_map/all_gather | solution.py:99
  248.8 23.7 %reduce_sum.18 = f32[64,1152]{1,0:T(8,128)S(1)} reduce(f32[256,64,1152]{2,1,0:T(8,128)} %bitcast.10, f32[]{:T(128)} %constant.20.clone.1), dimensions={0}, to_apply=%region_0.0 | reduce | flops 18800640 | bytes 75792384 | tf_op jit(solution)/shard_map/reduce_sum | solution.py:100
  273.4 3.7 %fusion = f32[2,3,4096]{2,1,0:T(4,128)S(1)} fusion(bf16[2,3,384]{2,1,0:T(4,128)(2,1)S(1)} %reshape.31, bf16[1,1,1,2,384,4096]{5,4,3,2,1,0:T(8,128)(2,1)} %param.8), kind=kOutput, calls=%fused_computation.1 | convolution fusion | flops 18874368 | bytes 6394368 | tf_op jit(solution)/shard_map/axz,ahx->ahz/dot_general | solution.py:105
  277.1 1.5 fusion.19
  278.7 0.5 copy.41
  279.3 0.6 copy-done.12
  280.5 2.4 bitcast_add_fusion
  (60 shorter events, 2.4 us)
Async XLA Ops:
  7.2 4.7 %copy-start.18 = (s32[1,1,1,2]{3,2,1,0:T(1,128)S(1)}, s32[1,1,1,2]{3,2,1,0:T(1,128)}, u32[]{:S(2)}) copy-start(s32[1,1,1,2]{3,2,1,0:T(1,128)} %param.7) | copy-start | bytes 28
  7.2 241.6 %all-gather.3.cloned.1.call-start = ((), (), s32[]{:S(2)}) async-start(), calls=%async_computation | async-start | bytes 75792384 | tf_op jit(solution)/shard_map/all_gather | solution.py:99
  14.8 4.5 %copy-start.17 = (s32[1,1,1,2]{3,2,1,0:T(1,128)S(1)}, s32[1,1,1,2]{3,2,1,0:T(1,128)}, u32[]{:S(2)}) copy-start(s32[1,1,1,2]{3,2,1,0:T(1,128)} %param.6) | copy-start | bytes 28
  21.4 5.6 %collective-permute-start = (f32[3,1,32,128]{3,2,1,0:T(8,128)S(1)}, f32[3,1,32,128]{3,2,1,0:T(8,128)S(1)}, u32[]{:S(2)}, u32[]{:S(2)}) collective-permute-start(f32[3,1,32,128]{3,2,1,0:T(8,128)S(1)} %get-tuple-element.16), channel_id=1, source_target_pairs={{0,16},{16,32},{32,48},{48,64},{64,80},{80,96},{96,112},{112,128},... | collective-permute-start | bytes 147464 | tf_op jit(solution)/shard_map/ppermute | solution.py:15
  23.3 5.9 %collective-permute-start.1 = (f32[3,1,32,128]{3,2,1,0:T(8,128)S(1)}, f32[3,1,32,128]{3,2,1,0:T(8,128)S(1)}, u32[]{:S(2)}, u32[]{:S(2)}) collective-permute-start(f32[3,1,32,128]{3,2,1,0:T(8,128)S(1)} %get-tuple-element.15), channel_id=1, source_target_pairs={{16,0},{32,16},{48,32},{64,48},{80,64},{96,80},{112,96},{128,112},... | collective-permute-start | bytes 147464 | tf_op jit(solution)/shard_map/ppermute | solution.py:18
  29.2 3.9 %copy-start.4 = (f32[3,66,32,128]{3,2,1,0:T(8,128)}, f32[3,66,32,128]{3,2,1,0:T(8,128)S(1)}, u32[]{:S(2)}) copy-start(f32[3,66,32,128]{3,2,1,0:T(8,128)S(1)} %constant_dynamic-update-slice_fusion) | copy-start | bytes 9732100
  35.9 7.5 %collective-permute-start.2 = (f32[3,66,32,1]{1,2,3,0:T(8,128)S(1)}, f32[3,66,32,1]{1,2,3,0:T(8,128)S(1)}, u32[]{:S(2)}, u32[]{:S(2)}) collective-permute-start(f32[3,66,32,1]{1,2,3,0:T(8,128)S(1)} %copy.27), channel_id=1, source_target_pairs={{0,4},{4,8},{8,12},{1,5},{5,9},{9,13},{2,6},{6,10},{10,14},{3,7},{... | collective-permute-start | bytes 76040 | tf_op jit(solution)/shard_map/ppermute | solution.py:15
  42.1 6.2 %collective-permute-start.3 = (f32[3,66,32,1]{1,2,3,0:T(8,128)S(1)}, f32[3,66,32,1]{1,2,3,0:T(8,128)S(1)}, u32[]{:S(2)}, u32[]{:S(2)}) collective-permute-start(f32[3,66,32,1]{1,2,3,0:T(8,128)S(1)} %copy.28), channel_id=1, source_target_pairs={{4,0},{8,4},{12,8},{5,1},{9,5},{13,9},{6,2},{10,6},{14,10},{7,3},{... | collective-permute-start | bytes 76040 | tf_op jit(solution)/shard_map/ppermute | solution.py:18
  50.9 16.9 %copy-start.5 = (f32[3,66,32,128]{3,2,1,0:T(8,128)S(1)}, f32[3,66,32,128]{3,2,1,0:T(8,128)}, u32[]{:S(2)}) copy-start(f32[3,66,32,128]{3,2,1,0:T(8,128)} %copy-done.4) | copy-start | bytes 9732100
  50.9 16.9 %copy-start.8 = (f32[3,66,32,1]{3,2,1,0:T(8,128)S(1)}, f32[3,66,32,1]{3,2,1,0:T(8,128)}, u32[]{:S(2)}) copy-start(f32[3,66,32,1]{3,2,1,0:T(8,128)} %copy.29) | copy-start | bytes 76036
  50.9 16.9 %copy-start.9 = (f32[3,66,32,1]{3,2,1,0:T(8,128)S(1)}, f32[3,66,32,1]{3,2,1,0:T(8,128)}, u32[]{:S(2)}) copy-start(f32[3,66,32,1]{3,2,1,0:T(8,128)} %copy.30) | copy-start | bytes 76036
  54.8 8.9 %collective-permute-start.4 = (f32[3,66,1,130]{3,2,1,0:T(1,128)S(1)}, f32[3,66,1,130]{3,2,1,0:T(1,128)S(1)}, u32[]{:S(2)}, u32[]{:S(2)}) collective-permute-start(f32[3,66,1,130]{3,2,1,0:T(1,128)S(1)} %get-tuple-element.6), channel_id=1, source_target_pairs={{0,1},{1,2},{2,3},{4,5},{5,6},{6,7},{8,9},{9,10},{10,11},{12,13},{... | collective-permute-start | bytes 308888 | tf_op jit(solution)/shard_map/ppermute | solution.py:15
  58.6 9.3 %collective-permute-start.5 = (f32[3,66,1,130]{3,2,1,0:T(1,128)S(1)}, f32[3,66,1,130]{3,2,1,0:T(1,128)S(1)}, u32[]{:S(2)}, u32[]{:S(2)}) collective-permute-start(f32[3,66,1,130]{3,2,1,0:T(1,128)S(1)} %get-tuple-element.7), channel_id=1, source_target_pairs={{1,0},{2,1},{3,2},{5,4},{6,5},{7,6},{9,8},{10,9},{11,10},{13,12},{... | collective-permute-start | bytes 308888 | tf_op jit(solution)/shard_map/ppermute | solution.py:18
  72.4 4.8 %copy-start = (f32[66,34,130]{2,1,0:T(8,128)}, f32[66,34,130]{2,1,0:T(8,128)S(1)}, u32[]{:S(2)}) copy-start(f32[66,34,130]{2,1,0:T(8,128)S(1)} %get-tuple-element.9) | copy-start | bytes 3500644
  72.4 4.8 %copy-start.2 = (f32[66,34,130]{2,1,0:T(8,128)}, f32[66,34,130]{2,1,0:T(8,128)S(1)}, u32[]{:S(2)}) copy-start(f32[66,34,130]{2,1,0:T(8,128)S(1)} %get-tuple-element.10) | copy-start | bytes 3500644
  77.2 9.0 %copy-start.6 = (f32[64,32,128]{2,1,0:T(8,128)}, f32[64,32,128]{2,1,0:T(8,128)S(1)}, u32[]{:S(2)}) copy-start(f32[64,32,128]{2,1,0:T(8,128)S(1)} %sqrt_add_fusion) | copy-start | bytes 3145732
  77.3 5.6 %collective-permute-start.7 = (f32[1,32,128]{2,1,0:T(8,128)S(1)}, f32[1,32,128]{2,1,0:T(8,128)S(1)}, u32[]{:S(2)}, u32[]{:S(2)}) collective-permute-start(f32[1,32,128]{2,1,0:T(8,128)S(1)} %get-tuple-element.19), channel_id=1, source_target_pairs={{0,16},{16,32},{32,48},{48,64},{64,80},{80,96},{96,112},{112,128},... | collective-permute-start | bytes 49160 | tf_op jit(solution)/shard_map/ppermute | solution.py:15
  79.2 5.1 %collective-permute-start.6 = (f32[1,32,128]{2,1,0:T(8,128)S(1)}, f32[1,32,128]{2,1,0:T(8,128)S(1)}, u32[]{:S(2)}, u32[]{:S(2)}) collective-permute-start(f32[1,32,128]{2,1,0:T(8,128)S(1)} %get-tuple-element.20), channel_id=1, source_target_pairs={{16,0},{32,16},{48,32},{64,48},{80,64},{96,80},{112,96},{128,112},... | collective-permute-start | bytes 49160 | tf_op jit(solution)/shard_map/ppermute | solution.py:18
  88.1 6.6 %collective-permute-start.9 = (f32[66,32,1]{0,1,2:T(8,128)S(1)}, f32[66,32,1]{0,1,2:T(8,128)S(1)}, u32[]{:S(2)}, u32[]{:S(2)}) collective-permute-start(f32[66,32,1]{0,1,2:T(8,128)S(1)} %copy.33), channel_id=1, source_target_pairs={{0,4},{4,8},{8,12},{1,5},{5,9},{9,13},{2,6},{6,10},{10,14},{3,7},{... | collective-permute-start | bytes 25352 | tf_op jit(solution)/shard_map/ppermute | solution.py:15
  93.4 6.1 %collective-permute-start.8 = (f32[66,32,1]{0,1,2:T(8,128)S(1)}, f32[66,32,1]{0,1,2:T(8,128)S(1)}, u32[]{:S(2)}, u32[]{:S(2)}) collective-permute-start(f32[66,32,1]{0,1,2:T(8,128)S(1)} %copy.31), channel_id=1, source_target_pairs={{4,0},{8,4},{12,8},{5,1},{9,5},{13,9},{6,2},{10,6},{14,10},{7,3},{... | collective-permute-start | bytes 25352 | tf_op jit(solution)/shard_map/ppermute | solution.py:18
  101.5 12.4 %copy-start.1 = (f32[66,34,130]{2,1,0:T(8,128)S(1)}, f32[66,34,130]{2,1,0:T(8,128)}, u32[]{:S(2)}) copy-start(f32[66,34,130]{2,1,0:T(8,128)} %copy-done) | copy-start | bytes 3500644
  103.5 5.4 %collective-permute-start.11 = (f32[66,1,130]{2,1,0:T(1,128)S(1)}, f32[66,1,130]{2,1,0:T(1,128)S(1)}, u32[]{:S(2)}, u32[]{:S(2)}) collective-permute-start(f32[66,1,130]{2,1,0:T(1,128)S(1)} %get-tuple-element.11), channel_id=1, source_target_pairs={{0,1},{1,2},{2,3},{4,5},{5,6},{6,7},{8,9},{9,10},{10,11},{12,13},{... | collective-permute-start | bytes 102968 | tf_op jit(solution)/shard_map/ppermute | solution.py:15
  106.9 19.4 %copy-start.3 = (f32[66,34,130]{2,1,0:T(8,128)S(1)}, f32[66,34,130]{2,1,0:T(8,128)}, u32[]{:S(2)}) copy-start(f32[66,34,130]{2,1,0:T(8,128)} %copy-done.2) | copy-start | bytes 3500644
  106.9 19.4 %copy-start.7 = (f32[64,32,128]{2,1,0:T(8,128)S(1)}, f32[64,32,128]{2,1,0:T(8,128)}, u32[]{:S(2)}) copy-start(f32[64,32,128]{2,1,0:T(8,128)} %copy-done.6) | copy-start | bytes 3145732
  107.0 19.4 %copy-start.10 = (f32[66,32,1]{2,1,0:T(8,128)S(1)}, f32[66,32,1]{2,1,0:T(8,128)}, u32[]{:S(2)}) copy-start(f32[66,32,1]{2,1,0:T(8,128)} %copy.34) | copy-start | bytes 25348
  107.0 19.4 %copy-start.11 = (f32[66,32,1]{2,1,0:T(8,128)S(1)}, f32[66,32,1]{2,1,0:T(8,128)}, u32[]{:S(2)}) copy-start(f32[66,32,1]{2,1,0:T(8,128)} %copy.32) | copy-start | bytes 25348
  107.0 6.9 %collective-permute-start.10 = (f32[66,1,130]{2,1,0:T(1,128)S(1)}, f32[66,1,130]{2,1,0:T(1,128)S(1)}, u32[]{:S(2)}, u32[]{:S(2)}) collective-permute-start(f32[66,1,130]{2,1,0:T(1,128)S(1)} %get-tuple-element.12), channel_id=1, source_target_pairs={{1,0},{2,1},{3,2},{5,4},{6,5},{7,6},{9,8},{10,9},{11,10},{13,12},{... | collective-permute-start | bytes 102968 | tf_op jit(solution)/shard_map/ppermute | solution.py:18
  248.8 24.2 %copy-start.16 = (f32[64,384]{1,0:T(8,128)S(1)}, f32[64,384]{1,0:T(8,128)}, u32[]{:S(2)}) copy-start(f32[64,384]{1,0:T(8,128)} %param.9) | copy-start | bytes 294916
  273.2 4.0 %copy-start.15 = (f32[64,1152]{1,0:T(8,128)}, f32[64,1152]{1,0:T(8,128)S(1)}, u32[]{:S(2)}) copy-start(f32[64,1152]{1,0:T(8,128)S(1)} %mul.301) | copy-start | bytes 884740
  278.7 1.2 copy-start.12
  278.7 1.5 copy-start.13
  278.7 1.8 copy-start.14
Sparse Core Ops, SparseCore 0:
  20.6 228.1 all-gather.2
